TPU v7x, 32 devices: a whole 2x2x4 slice. The times are simulated.
32 devices in a mesh: grp: 4 (over y, core), rows: 8 (over z, x).
Axes of the slice: x: 2, y: 2, z: 4, core: 2. Of those that a mesh axis runs over, the one named last changes fastest.
Arguments:
- rhs: float32 [2048, 64, 128], P(('grp', 'rows')), may hold values from -6 to 6
- fine_diag: bfloat16 [2048, 64, 64], P(('grp', 'rows')), may hold values from -0.2 to 1.2
- fine_smoother: bfloat16 [2048, 64, 64], P(('grp', 'rows')), may hold values from -4 to 4
- fine_blocks: bfloat16 [2048, 7, 64, 64], P(('grp', 'rows')), may hold values from -0.1796875 to 0.1796875
- fine_cols: int32 [2048, 7], P(('grp', 'rows')), may hold values from 0 to 2047, as said below
- aggregate: int32 [2048], P(('grp', 'rows')), may hold values from 0 to 511, as said below
- coarse_diag: bfloat16 [512, 64, 64], P('rows'), may hold values from -0.8 to 4.8
- coarse_smoother: bfloat16 [512, 64, 64], P('rows'), may hold values from -1 to 1
- coarse_blocks: bfloat16 [512, 7, 64, 64], P('rows'), may hold values from -0.71875 to 0.71875
- coarse_cols: int32 [512, 7], P('rows'), may hold values from 0 to 511, as said below
Outputs:
- solution: float32 [2048, 64, 128], P(('grp', 'rows'))
Inputs may be any that keep to these rules, and one draw needn't show every extreme that they name: fine_cols row i names rows within 32 of i; the distance 32 is reached. coarse_cols row c names rows within 32 of c; the distance 32 is reached. `aggregate`: aggregate_i lies in [r * 64, (r + 1) * 64) with r = (i // 64) mod 8.
All inputs are finite; a program needn't handle non-finite values.
Results may differ from a plain program's by a relative error of at most 0.001.
The roundings to bfloat16 on the way count: a program that leaves them out, or rounds other values in their place, can miss the bound.
Values may be sent and summed in bfloat16 or wider, within the bound.
A program may use at most 128 MiB of HBM per device.

v0:
```python
import functools

import jax
import jax.numpy as jnp
from jax import lax
from jax.experimental import pallas as pl
from jax.experimental.pallas import tpu as pltpu
from jax.sharding import PartitionSpec as P

MESH = pl.DeviceIdType.MESH
damping = 0.8
steps = 8
early = 1
parts = 4
low = jnp.bfloat16
f32 = jnp.float32


def dot(a, b):
    return jnp.dot(a, b, preferred_element_type=f32)


def row_product(i, columns, at, base, offs, diag, extended, own):
    count = offs.shape[1]
    last = extended.shape[0] - 1
    vectors = [extended[jnp.clip(columns[k, at] - base, 0, last)] for k in range(count)] + [extended[own]]
    blocks = [offs[i, k] for k in range(count)] + [diag[i]]
    total = None
    for p in range(0, count + 1, 4):
        term = dot(
            jnp.concatenate(blocks[p : p + 4], axis=1),
            jnp.concatenate(vectors[p : p + 4], axis=0),
        )
        total = term if total is None else total + term
    return total


def kernel(
    groups, ranks,
    fine_cols, coarse_cols, aggregate,
    rhs_hbm, diag_hbm, smoother_hbm, blocks_hbm, cdiag_hbm, csmoother_hbm, cblocks_hbm,
    iterate_hbm, correction_hbm,
    rhs, diag, smoother, blocks, cdiag, csmoother, cblocks,
    ext1, ext2, landing1, landing2, iterate, sums, partial, from_partner, chip_send, chip_recv, crhs, cfirst, cext, correction, chain,
    load_sem, out_sem, halo_send, halo_recv, rs_send, rs_recv, rc_send, rc_recv,
    piece_send, piece_recv, ag_send, ag_recv, fwd_send, fwd_recv,
):
    g = lax.axis_index("grp")
    r = lax.axis_index("rows")
    height = rhs.shape[0]
    margin = height // 2
    cheight = partial.shape[0]
    piece = cheight // groups
    chips = groups // 2
    reach = groups // 2
    chunk = margin // steps
    share = piece // parts

    flat = g * ranks + r
    has_left = flat > 0
    has_right = flat < groups * ranks - 1
    left = ((flat - 1) // ranks, (flat + ranks - 1) % ranks)
    right = ((flat + 1) // ranks, (flat + 1) % ranks)
    core = g % 2
    chip = g // 2
    partner = (chip * 2 + 1 - core, r)

    def piece_of(group, rank):
        odd = rank % 2
        return odd * (groups - 1 - group) + (1 - odd) * group

    q = piece_of(g, r)
    linear = r * groups + q

    def holder(index):
        rank = index // groups
        return (piece_of(index % groups, rank), rank)

    def chip_peer(o):
        return (((chip + o) % chips) * 2 + core, r)

    shifts = [d for s in range(1, reach + 1) for d in (s, -s)]

    def exists(index):
        return jnp.logical_and(index >= 0, index < groups * ranks)

    def load(src, dst, at):
        return pltpu.make_async_copy(src, dst, load_sem.at[at])

    mine = pl.ds(q * piece, piece)
    first_loads = [load(rhs_hbm, rhs, 0), load(smoother_hbm, smoother, 1)]
    later_loads = [
        load(blocks_hbm, blocks, 2),
        load(diag_hbm, diag, 3),
        load(csmoother_hbm.at[mine], csmoother, 4),
        load(cdiag_hbm.at[mine], cdiag, 5),
        load(cblocks_hbm.at[mine], cblocks, 6),
    ]
    for c in first_loads:
        c.start()

    barrier = pltpu.get_barrier_semaphore()

    def greet(device):
        pl.semaphore_signal(barrier, inc=1, device_id=device, device_id_type=MESH)

    pl.when(has_left)(lambda: greet(left))
    pl.when(has_right)(lambda: greet(right))
    greet(partner)
    for o in range(1, chips):
        greet(chip_peer(o))
    met = 1 + chips - 1 + has_left.astype(jnp.int32) + has_right.astype(jnp.int32)
    for d in shifts:
        there = exists(linear + d)
        pl.when(there)(functools.partial(lambda d: greet(holder(linear + d)), d))
        met = met + there.astype(jnp.int32)
    pl.semaphore_wait(barrier, met)

    def remote(src, dst, send, recv, device):
        return pltpu.make_async_remote_copy(
            src_ref=src, dst_ref=dst, send_sem=send, recv_sem=recv, device_id=device, device_id_type=MESH
        )

    def to_right(ext, phase, j):
        src = ext.at[pl.ds(margin + height - (j + 1) * chunk, chunk)]
        at = pl.ds(margin - (j + 1) * chunk, chunk)
        dst = (landing1, landing2)[phase].at[0, at]
        return remote(src, dst, halo_send.at[phase, 0, j], halo_recv.at[phase, 0, j], right)

    def to_left(ext, phase, j):
        src = ext.at[pl.ds(margin + j * chunk, chunk)]
        at = pl.ds(j * chunk, chunk)
        dst = (landing1, landing2)[phase].at[1, at]
        return remote(src, dst, halo_send.at[phase, 1, j], halo_recv.at[phase, 1, j], left)

    def send_halo(ext, phase, j):
        pl.when(has_right)(lambda: to_right(ext, phase, j).start())
        pl.when(has_left)(lambda: to_left(ext, phase, j).start())

    def wait_halo(ext, phase, j):
        pl.when(has_left)(lambda: to_right(ext, phase, j).wait_recv())
        pl.when(has_right)(lambda: to_left(ext, phase, j).wait_recv())

    def wait_sent(ext, phase, j):
        pl.when(has_right)(lambda: to_right(ext, phase, j).wait_send())
        pl.when(has_left)(lambda: to_left(ext, phase, j).wait_send())

    def rows(start, count, body, unroll):
        def step(n, carry):
            body(start + n)
            return carry

        lax.fori_loop(0, count, step, 0, unroll=unroll)

    for c in first_loads:
        c.wait()

    def first(i):
        value = damping * dot(smoother[i], rhs[i].astype(low))
        iterate[i] = value
        ext1[margin + i] = value.astype(low)

    for j in range(steps):
        rows(height - (j + 1) * chunk, chunk, first, 4)
        rows(j * chunk, chunk, first, 4)
        send_halo(ext1, 0, j)
    for c in later_loads:
        c.start()
    starts = [at for j in range(steps) for at in (margin - (j + 1) * chunk, margin + j * chunk)]

    def earlier(wanted, runs):
        found = jnp.int32(0)
        for n in range(runs):
            for m in range(chunk):
                found = jnp.where(aggregate[starts[n] + m] == wanted, 1 + n * chunk + m, found)
        return found

    def link_run(n):
        def link(m):
            wanted = aggregate[starts[n] + m]
            found = earlier(wanted, n)
            for k in range(chunk - 1):
                same = jnp.logical_and(aggregate[starts[n] + k] == wanted, k < m)
                found = jnp.where(same, 1 + n * chunk + k, found)
            chain[starts[n] + m] = found

        rows(0, chunk, link, 1)

    def link_coarse(c):
        chain[height + c] = earlier(r * cheight + c, len(starts))

    def place(ext, landing, j):
        def place_low(i):
            ext[i] = landing[0, i]

        def place_high(i):
            ext[margin + height + i] = landing[1, i]

        pl.when(has_left)(lambda: rows(margin - (j + 1) * chunk, chunk, place_low, 4))
        pl.when(has_right)(lambda: rows(j * chunk, chunk, place_high, 4))

    rows(0, cheight // 2, link_coarse, 1)
    later_loads[0].wait()
    later_loads[1].wait()

    base = flat * height - margin

    def second(i):
        residual = rhs[i] - row_product(i, fine_cols, i, base, blocks, diag, ext1, margin + i)
        value = iterate[i] + damping * dot(smoother[i], residual.astype(low))
        iterate[i] = value
        ext2[margin + i] = value.astype(low)

    for j in range(steps):
        wait_halo(ext1, 0, j)
        place(ext1, landing1, j)
        rows(margin - (j + 1) * chunk, chunk, second, 2)
        rows(margin + j * chunk, chunk, second, 2)
        if j < early:
            send_halo(ext2, 1, steps - 1 - j)
        if j < steps - 1:
            link_run(2 * j)
            link_run(2 * j + 1)
    for j in range(steps - early):
        send_halo(ext2, 1, j)
    keep_iterate = pltpu.make_async_copy(iterate, iterate_hbm, load_sem.at[7])
    keep_iterate.start()
    link_run(2 * steps - 2)
    link_run(2 * steps - 1)

    sums[0] = jnp.zeros(sums.shape[1:], f32)

    def third(shift):
        def body(i):
            residual = rhs[i] - row_product(i, fine_cols, i, base, blocks, diag, ext2, margin + i)
            sums[i + shift] = residual + sums[chain[i]]

        return body

    for j in reversed(range(steps - early, steps)):
        wait_halo(ext2, 1, j)
        place(ext2, landing2, j)
    for j in range(steps):
        if j < steps - early:
            wait_halo(ext2, 1, j)
            place(ext2, landing2, j)
        for n, start in enumerate((margin - (j + 1) * chunk, margin + j * chunk)):
            rows(start, chunk, third(1 + (2 * j + n) * chunk - start), 2)
        if j < 4:
            rows(cheight // 2 + j * (cheight // 8), cheight // 8, link_coarse, 1)

    def gather(c):
        partial[c] = sums[chain[height + c]]

    rows(0, cheight, gather, 4)

    def slice_of(group, p):
        return pl.ds(piece_of(group, r) * piece + p * share, share)

    def to_partner(o, p):
        src = partial.at[slice_of(((chip + o) % chips) * 2 + 1 - core, p)]
        dst = from_partner.at[o, pl.ds(p * share, share)]
        return remote(src, dst, rs_send.at[o, p], rs_recv.at[o, p], partner)

    order = [*range(1, chips), 0]
    for o in order:
        for p in range(parts):
            to_partner(o, p).start()

    def across(o, p):
        at = pl.ds(p * share, share)
        return remote(chip_send.at[o, at], chip_recv.at[o, at], rc_send.at[o, p], rc_recv.at[o, p], chip_peer(o))

    for o in order:
        start = piece_of(((chip + o) % chips) * 2 + core, r) * piece

        def pack(n):
            chip_send[o, n] = (partial[start + n] + from_partner[o, n]).astype(low)

        def keep(n):
            crhs[n] = partial[start + n] + from_partner[o, n]

        for p in range(parts):
            to_partner(o, p).wait_recv()
            rows(p * share, share, pack if o else keep, 2)
            if o:
                across(o, p).start()
    for c in later_loads[2:]:
        c.wait()

    def coarse_first(n):
        total = crhs[n]
        for o in range(1, chips):
            total = total + chip_recv[o, n].astype(f32)
        crhs[n] = total
        value = damping * dot(csmoother[n], total.astype(low))
        cfirst[n] = value
        cext[reach * piece + n] = value.astype(low)

    def to_shift(d, p):
        at = shifts.index(d)
        return remote(
            cext.at[pl.ds(reach * piece + p * share, share)], cext.at[pl.ds((reach - d) * piece + p * share, share)],
            piece_send.at[at, p], piece_recv.at[at, p], holder(linear + d),
        )

    def each_part(method, d):
        for p in range(parts):
            getattr(to_shift(d, p), method)()

    for p in range(parts):
        for o in range(1, chips):
            across(o, p).wait_recv()
        rows(p * share, share, coarse_first, 2)
        for d in reversed(shifts):
            pl.when(exists(linear + d))(functools.partial(lambda d: to_shift(d, p).start(), d))
    for d in reversed(shifts):
        pl.when(exists(linear - d))(functools.partial(each_part, "wait_recv", d))

    cbase = (linear - reach) * piece

    def coarse_second(n):
        image = row_product(n, coarse_cols, q * piece + n, cbase, cblocks, cdiag, cext, reach * piece + n)
        value = cfirst[n] + damping * dot(csmoother[n], (crhs[n] - image).astype(low))
        correction[q * piece + n] = value.astype(low)

    def piece_to(o, p):
        at = slice_of(g, p)
        return remote(correction.at[at], correction.at[at], ag_send.at[o, p], ag_recv.at[o, p], chip_peer(o))

    def forward(o, p):
        at = slice_of(((chip + o) % chips) * 2 + core, p)
        return remote(correction.at[at], correction.at[at], fwd_send.at[o, p], fwd_recv.at[o, p], partner)

    def put(o, own, p):
        at = slice_of(((chip + o) % chips) * 2 + (core if own else 1 - core), p)
        return pltpu.make_async_copy(correction.at[at], correction_hbm.at[at], out_sem.at[o, own, p])

    for p in range(parts):
        rows(p * share, share, coarse_second, 2)
        for o in range(1, chips):
            piece_to(o, p).start()
        forward(0, p).start()
        put(0, 1, p).start()
    for o in range(1, chips):
        for p in range(parts):
            piece_to(o, p).wait_recv()
            forward(chips - o, p).start()
            put(chips - o, 1, p).start()
    for o in [0, *reversed(range(1, chips))]:
        for p in range(parts):
            forward(o, p).wait_recv()
            put(o, 0, p).start()

    for j in range(steps):
        wait_sent(ext1, 0, j)
        wait_sent(ext2, 1, j)
    for p in range(parts):
        for o in range(chips):
            to_partner(o, p).wait_send()
            forward(o, p).wait_send()
            put(o, 0, p).wait()
            put(o, 1, p).wait()
        for o in range(1, chips):
            across(o, p).wait_send()
            piece_to(o, p).wait_send()
    for d in shifts:
        pl.when(exists(linear + d))(functools.partial(each_part, "wait_send", d))
    keep_iterate.wait()


def add_kernel(
    cheight, aggregate, iterate_hbm, correction_hbm, out_hbm, iterate, correction, in_sem, correction_sem, out_sem
):
    share = iterate.shape[0] // 4
    cshare = cheight // 4
    start = lax.axis_index("rows") * cheight

    def fetch(j):
        at = pl.ds(j * cshare, cshare)
        return pltpu.make_async_copy(correction_hbm.at[at], correction.at[at], correction_sem.at[j])

    def get(j):
        at = pl.ds(j * share, share)
        return pltpu.make_async_copy(iterate_hbm.at[at], iterate.at[at], in_sem.at[j])

    def put(j):
        at = pl.ds(j * share, share)
        return pltpu.make_async_copy(iterate.at[at], out_hbm.at[at], out_sem.at[j])

    for j in range(4):
        fetch(j).start()
    for j in range(4):
        get(j).start()
    for j in range(4):
        fetch(j).wait()
    for j in range(4):
        get(j).wait()

        def step(n, carry):
            i = j * share + n
            iterate[i] = iterate[i] + correction[aggregate[i] - start].astype(f32)
            return carry

        lax.fori_loop(0, share, step, 0, unroll=4)
        put(j).start()
    for j in range(4):
        put(j).wait()


def on_device(
    groups, ranks,
    rhs, fine_diag, fine_smoother, fine_blocks, fine_cols, aggregate,
    coarse_diag, coarse_smoother, coarse_blocks, coarse_cols,
):
    height, b, n = rhs.shape
    cheight = coarse_diag.shape[0]
    neighbours = fine_blocks.shape[1]
    piece = cheight // groups
    chips = groups // 2
    reach = groups // 2
    vmem = pltpu.VMEM
    dma = pltpu.SemaphoreType.DMA
    smem = pl.BlockSpec(memory_space=pltpu.SMEM)
    hbm = pl.BlockSpec(memory_space=pl.ANY)
    iterate, correction = pl.pallas_call(
        functools.partial(kernel, groups, ranks),
        out_shape=(jax.ShapeDtypeStruct(rhs.shape, f32), jax.ShapeDtypeStruct((cheight, b, n), low)),
        in_specs=[smem] * 3 + [hbm] * 7,
        out_specs=(hbm, hbm),
        scratch_shapes=[
            vmem((height, b, n), f32),
            vmem((height, b, b), low),
            vmem((height, b, b), low),
            vmem((height, neighbours, b, b), low),
            vmem((piece, b, b), low),
            vmem((piece, b, b), low),
            vmem((piece, neighbours, b, b), low),
            vmem((2 * height, b, n), low),
            vmem((2 * height, b, n), low),
            vmem((2, height // 2, b, n), low),
            vmem((2, height // 2, b, n), low),
            vmem((height, b, n), f32),
            vmem((height + 1, b, n), f32),
            vmem((cheight, b, n), f32),
            vmem((chips, piece, b, n), f32),
            vmem((chips, piece, b, n), low),
            vmem((chips, piece, b, n), low),
            vmem((piece, b, n), f32),
            vmem((piece, b, n), f32),
            vmem(((2 * reach + 1) * piece, b, n), low),
            vmem((cheight, b, n), low),
            pltpu.SMEM((height + cheight,), jnp.int32),
            dma((8,)),
            dma((chips, 2, parts)),
            dma((2, 2, steps)),
            dma((2, 2, steps)),
            dma((chips, parts)),
            dma((chips, parts)),
            dma((chips, parts)),
            dma((chips, parts)),
            dma((2 * reach, parts)),
            dma((2 * reach, parts)),
            dma((chips, parts)),
            dma((chips, parts)),
            dma((chips, parts)),
            dma((chips, parts)),
        ],
        compiler_params=pltpu.CompilerParams(
            collective_id=0, has_side_effects=True, vmem_limit_bytes=60 * 1024 * 1024
        ),
        name="cycle",
    )(
        fine_cols.T, coarse_cols.T, aggregate,
        rhs, fine_diag, fine_smoother, fine_blocks, coarse_diag, coarse_smoother, coarse_blocks,
    )
    return pl.pallas_call(
        functools.partial(add_kernel, cheight),
        out_shape=jax.ShapeDtypeStruct(rhs.shape, f32),
        in_specs=[smem, hbm, hbm],
        out_specs=hbm,
        scratch_shapes=[vmem((height, b, n), f32), vmem((cheight, b, n), low), dma((4,)), dma((4,)), dma((4,))],
        name="add",
    )(aggregate, iterate, correction)


def solution(mesh):
    fine = P(("grp", "rows"))
    return jax.shard_map(
        functools.partial(on_device, mesh.shape["grp"], mesh.shape["rows"]),
        mesh=mesh,
        in_specs=(fine,) * 6 + (P("rows"),) * 4,
        out_specs=fine,
        check_vma=False,
    )
```

profile of v0, /device:TPU:3, one launch (start us, length us, event | category | flops | bytes accessed | tf_op | source)
XLA Modules:
  0.0 90.4 jit_solution(15751525644038181614)
XLA Ops:
  0.0 86.6 %cycle.1 = (f32[64,64,128]{2,1,0:T(8,128)}, bf16[64,64,128]{2,1,0:T(8,128)(2,1)}) custom-call(s32[7,64]{1,0:T(8,128)} %bitcast.2, s32[7,64]{1,0:T(8,128)} %bitcast.3, s32[64]{0:T(128)} %aggregate.3, f32[64,64,128]{2,1,0:T(8,128)} %rhs_hbm.1, bf16[64,64,64]{2,1,0:T(8,128)(2,1)} %diag_hbm.1, bf16[64,64,64]{2,1,0:T(8,128)(2,1)} %smoother_hbm.1, ...), custom_call_target="tpu_custom_call" | custom-call | tf_op jit(solution)/shard_map/cycle/pallas_call | solution.py:426
  86.6 3.8 %add.1 = f32[64,64,128]{2,1,0:T(8,128)} custom-call(s32[64]{0:T(128)} %aggregate.3, f32[64,64,128]{2,1,0:T(8,128)} %get-tuple-element.7.iterate_hbm, bf16[64,64,128]{2,1,0:T(8,128)(2,1)} %get-tuple-element.8.correction_hbm), custom_call_target="tpu_custom_call" | custom-call | tf_op jit(solution)/shard_map/add/pallas_call | solution.py:477
where the time goes:
time: 91.6 us; the launch traced here: 90.4 us
  Pallas kernels  90.4 us (99%)
    pallas_call x1, Pallas kernels, on_device(): pl.pallas_call(functools.partial(kernel, groups, ranks), out_shape=(jax.S...  86.6 us
    pallas_call x1, Pallas kernels, on_device(): pl.pallas_call(functools.partial(add_kernel, cheight), out_shape=jax.Shap...  3.8 us

commit v1 on v0

--- a/solution.py
+++ b/solution.py
@@ -10,7 +10,7 @@
 MESH = pl.DeviceIdType.MESH
 damping = 0.8
 steps = 8
-early = 1
+depth = 3
 parts = 4
 low = jnp.bfloat16
 f32 = jnp.float32
@@ -114,7 +114,6 @@
         there = exists(linear + d)
         pl.when(there)(functools.partial(lambda d: greet(holder(linear + d)), d))
         met = met + there.astype(jnp.int32)
-    pl.semaphore_wait(barrier, met)
 
     def remote(src, dst, send, recv, device):
         return pltpu.make_async_remote_copy(
@@ -154,18 +153,30 @@
 
     for c in first_loads:
         c.wait()
+    for c in later_loads:
+        c.start()
 
     def first(i):
         value = damping * dot(smoother[i], rhs[i].astype(low))
         iterate[i] = value
         ext1[margin + i] = value.astype(low)
 
+    queue = [(ext1, 0, j) for j in range(steps)] + [(ext2, 1, steps - 1)] + [(ext2, 1, j) for j in range(steps - 1)]
+
+    def push(n):
+        if n >= depth:
+            wait_sent(*queue[n - depth])
+        send_halo(*queue[n])
+
     for j in range(steps):
         rows(height - (j + 1) * chunk, chunk, first, 4)
         rows(j * chunk, chunk, first, 4)
-        send_halo(ext1, 0, j)
-    for c in later_loads:
-        c.start()
+        if j == 1:
+            pl.semaphore_wait(barrier, met)
+            push(0)
+            push(1)
+        elif 1 < j < depth:
+            push(j)
     starts = [at for j in range(steps) for at in (margin - (j + 1) * chunk, margin + j * chunk)]
 
     def earlier(wanted, runs):
@@ -205,24 +216,29 @@
 
     base = flat * height - margin
 
+    def residual_low(i):
+        residual = rhs[i] - row_product(i, fine_cols, i, base, blocks, diag, ext1, margin + i)
+        ext2[margin + i] = residual.astype(low)
+
     def second(i):
-        residual = rhs[i] - row_product(i, fine_cols, i, base, blocks, diag, ext1, margin + i)
-        value = iterate[i] + damping * dot(smoother[i], residual.astype(low))
+        value = iterate[i] + damping * dot(smoother[i], ext2[margin + i])
         iterate[i] = value
         ext2[margin + i] = value.astype(low)
 
     for j in range(steps):
+        if j + depth <= steps:
+            push(j + depth)
         wait_halo(ext1, 0, j)
         place(ext1, landing1, j)
-        rows(margin - (j + 1) * chunk, chunk, second, 2)
-        rows(margin + j * chunk, chunk, second, 2)
-        if j < early:
-            send_halo(ext2, 1, steps - 1 - j)
+        rows(margin - (j + 1) * chunk, chunk, residual_low, 4)
+        rows(margin + j * chunk, chunk, residual_low, 4)
+        rows(margin - (j + 1) * chunk, chunk, second, 4)
+        rows(margin + j * chunk, chunk, second, 4)
         if j < steps - 1:
             link_run(2 * j)
             link_run(2 * j + 1)
-    for j in range(steps - early):
-        send_halo(ext2, 1, j)
+    for n in range(steps + 1, steps + depth):
+        push(n)
     keep_iterate = pltpu.make_async_copy(iterate, iterate_hbm, load_sem.at[7])
     keep_iterate.start()
     link_run(2 * steps - 2)
@@ -237,11 +253,12 @@
 
         return body
 
-    for j in reversed(range(steps - early, steps)):
-        wait_halo(ext2, 1, j)
-        place(ext2, landing2, j)
+    wait_halo(ext2, 1, steps - 1)
+    place(ext2, landing2, steps - 1)
     for j in range(steps):
-        if j < steps - early:
+        if steps + depth + j < 2 * steps:
+            push(steps + depth + j)
+        if j < steps - 1:
             wait_halo(ext2, 1, j)
             place(ext2, landing2, j)
         for n, start in enumerate((margin - (j + 1) * chunk, margin + j * chunk)):
@@ -352,9 +369,8 @@
             forward(o, p).wait_recv()
             put(o, 0, p).start()
 
-    for j in range(steps):
-        wait_sent(ext1, 0, j)
-        wait_sent(ext2, 1, j)
+    for n in range(2 * steps - depth, 2 * steps):
+        wait_sent(*queue[n])
     for p in range(parts):
         for o in range(chips):
             to_partner(o, p).wait_send()

time: 91.6 us -> 85.9 us (0.938)
  Pallas kernels: 90.4 us -> 85.2 us
    pallas_call x1, Pallas kernels: 86.6 us -> 81.4 us  [on_device(): pl.pallas_call(functools.partial(kernel, groups, ranks), out_shape=(jax.S...]
where the time goes in v1:
time: 85.9 us; the launch traced here: 85.2 us
  Pallas kernels  85.2 us (99%)
    pallas_call x1, Pallas kernels, on_device(): pl.pallas_call(functools.partial(kernel, groups, ranks), out_shape=(jax.S...  81.4 us
    pallas_call x1, Pallas kernels, on_device(): pl.pallas_call(functools.partial(add_kernel, cheight), out_shape=jax.Shap...  3.8 us

profile of v1, /device:TPU:3, one launch (start us, length us, event | category | flops | bytes accessed | tf_op | source)
XLA Modules:
  0.0 85.2 jit_solution(11993141505379036267)
XLA Ops:
  0.0 81.4 %cycle.1 = (f32[64,64,128]{2,1,0:T(8,128)}, bf16[64,64,128]{2,1,0:T(8,128)(2,1)}) custom-call(s32[7,64]{1,0:T(8,128)} %bitcast.2, s32[7,64]{1,0:T(8,128)} %bitcast.3, s32[64]{0:T(128)} %aggregate.3, f32[64,64,128]{2,1,0:T(8,128)} %rhs_hbm.1, bf16[64,64,64]{2,1,0:T(8,128)(2,1)} %diag_hbm.1, bf16[64,64,64]{2,1,0:T(8,128)(2,1)} %smoother_hbm.1, ...), custom_call_target="tpu_custom_call" | custom-call | tf_op jit(solution)/shard_map/cycle/pallas_call | solution.py:442
  81.4 3.8 %add.1 = f32[64,64,128]{2,1,0:T(8,128)} custom-call(s32[64]{0:T(128)} %aggregate.3, f32[64,64,128]{2,1,0:T(8,128)} %get-tuple-element.7.iterate_hbm, bf16[64,64,128]{2,1,0:T(8,128)(2,1)} %get-tuple-element.8.correction_hbm), custom_call_target="tpu_custom_call" | custom-call | tf_op jit(solution)/shard_map/add/pallas_call | solution.py:493

commit v2 on v1

v2 whole, which is shorter than its diff:
```python
import functools

import jax
import jax.numpy as jnp
from jax import lax
from jax.experimental import pallas as pl
from jax.experimental.pallas import tpu as pltpu
from jax.sharding import PartitionSpec as P

MESH = pl.DeviceIdType.MESH
damping = 0.8
lanes = 128
sublanes = 8
depth = 4
csub = 4
low = jnp.bfloat16
f32 = jnp.float32


def dot(a, b):
    return jnp.dot(a, b, preferred_element_type=f32)


def row_product(i, columns, at, base, offs, diag, extended, own):
    count = offs.shape[1]
    last = extended.shape[0] - 1
    vectors = [extended[jnp.clip(columns[k, at] - base, 0, last)] for k in range(count)] + [extended[own]]
    blocks = [offs[i, k] for k in range(count)] + [diag[i]]
    total = None
    for p in range(0, count + 1, 4):
        term = dot(
            jnp.concatenate(blocks[p : p + 4], axis=1),
            jnp.concatenate(vectors[p : p + 4], axis=0),
        )
        total = term if total is None else total + term
    return total


def absorb_order(groups, steps):
    lag = [0, 1] + [4 + k % 2 for k in range(2, groups)]
    return [(k, t - lag[k]) for t in range(steps + max(lag)) for k in range(groups) if 0 <= t - lag[k] < steps]


def kernel(
    groups, ranks,
    fine_cols, coarse_cols, aggregate,
    rhs_hbm, diag_hbm, smoother_hbm, blocks_hbm, cdiag_hbm, csmoother_hbm, cblocks_hbm,
    iterate,
    rhs, diag, smoother, blocks, cdiag, csmoother, cblocks,
    ext1, ext2, landing1, landing2,
    own_full, own_low, near_full, far_low, via_low, sums, names, tables, chain,
    cfirst, cres, cext, clanding, correction,
    load_sem, halo_send, halo_recv, name_sem, near_send, near_recv,
    far_send, far_recv, via_send, via_recv, cx_send, cx_recv, cf_send, cf_recv, cp_sem,
):
    g = lax.axis_index("grp")
    r = lax.axis_index("rows")
    height = rhs.shape[0]
    margin = height // 2
    steps = height // sublanes
    chunk = sublanes // 2
    piece = chunk // 2
    cheight = correction.shape[0]
    cmargin = cheight // 2
    chips = groups // 2
    parts = cmargin // (csub * chips)
    span = csub * chips

    flat = g * ranks + r
    has_left = flat > 0
    has_right = flat < groups * ranks - 1
    left = ((flat - 1) // ranks, (flat + ranks - 1) % ranks)
    right = ((flat + 1) // ranks, (flat + 1) % ranks)
    core = g % 2
    chip = g // 2
    partner = (chip * 2 + 1 - core, r)
    side = 1 - core
    forth = (g, r + 1 - 2 * core)
    can_send = jnp.where(core == 0, r < ranks - 1, r > 0)
    can_recv = jnp.where(core == 0, r > 0, r < ranks - 1)

    def peer(o, same):
        return (((chip + o) % chips) * 2 + (core if same else 1 - core), r)

    def load(src, dst, at):
        return pltpu.make_async_copy(src, dst, load_sem.at[at])

    mine = pl.ds(core * cmargin, cmargin)
    first_loads = [load(rhs_hbm, rhs, 0), load(smoother_hbm, smoother, 1)]
    later_loads = [
        load(blocks_hbm, blocks, 2),
        load(diag_hbm, diag, 3),
        load(csmoother_hbm, csmoother, 4),
        load(cdiag_hbm.at[mine], cdiag, 5),
        load(cblocks_hbm.at[mine], cblocks, 6),
    ]
    for c in first_loads:
        c.start()

    barrier = pltpu.get_barrier_semaphore()

    def greet(device):
        pl.semaphore_signal(barrier, inc=1, device_id=device, device_id_type=MESH)

    pl.when(has_left)(lambda: greet(left))
    pl.when(has_right)(lambda: greet(right))
    greet(partner)
    for o in range(1, chips):
        greet(peer(o, True))
        greet(peer(o, False))
    met = groups - 1 + has_left.astype(jnp.int32) + has_right.astype(jnp.int32)

    def remote(src, dst, send, recv, device):
        return pltpu.make_async_remote_copy(
            src_ref=src, dst_ref=dst, send_sem=send, recv_sem=recv, device_id=device, device_id_type=MESH
        )

    pieces = margin // piece
    queue = [(0, j * piece, piece) for j in range(pieces)] + [(1, margin - piece, piece)]
    queue += [(1, j * piece, piece) for j in range(pieces - 1)]
    second_queue = pieces + 1
    pushed = []
    exts, landings = (ext1, ext2), (landing1, landing2)

    def to_right(n, item=None):
        phase, start, count = item or queue[n]
        src = exts[phase].at[pl.ds(margin + height - start - count, count)]
        dst = landings[phase].at[0, pl.ds(margin - start - count, count)]
        return remote(src, dst, halo_send.at[0, n % depth], halo_recv.at[phase, 0, start // chunk], right)

    def to_left(n, item=None):
        phase, start, count = item or queue[n]
        src = exts[phase].at[pl.ds(margin + start, count)]
        dst = landings[phase].at[1, pl.ds(start, count)]
        return remote(src, dst, halo_send.at[1, n % depth], halo_recv.at[phase, 1, start // chunk], left)

    def wait_sent(n):
        pl.when(has_right)(lambda: to_right(n).wait_send())
        pl.when(has_left)(lambda: to_left(n).wait_send())

    def launch(n):
        if n >= depth:
            wait_sent(n - depth)
        pl.when(has_right)(lambda: to_right(n).start())
        pl.when(has_left)(lambda: to_left(n).start())

    def push(upto):
        while len(pushed) < min(upto, len(queue)):
            launch(len(pushed))
            pushed.append(None)

    def rows(start, count, body, unroll):
        def step(n, carry):
            body(start + n)
            return carry

        lax.fori_loop(0, count, step, 0, unroll=unroll)

    def wait_halo(phase, j):
        start, count = j * chunk, chunk
        pl.when(has_left)(lambda: to_right(0, (phase, start, count)).wait_recv())
        pl.when(has_right)(lambda: to_left(0, (phase, start, count)).wait_recv())
        ext, landing = exts[phase], landings[phase]

        def place_low(i):
            ext[i] = landing[0, i]

        def place_high(i):
            ext[margin + height + i] = landing[1, i]

        pl.when(has_left)(lambda: rows(margin - start - count, count, place_low, count))
        pl.when(has_right)(lambda: rows(start, count, place_high, count))

    starts = [at for j in range(steps) for at in (margin - (j + 1) * chunk, margin + j * chunk)]

    lane = lax.broadcasted_iota(jnp.int32, (sublanes, lanes), 1)
    sublane = lax.broadcasted_iota(jnp.int32, (sublanes, lanes), 0)
    named = jnp.zeros((sublanes, lanes), jnp.int32)
    for n, start in enumerate(starts):
        for m in range(chunk):
            named = jnp.where(lane == n * chunk + m, aggregate[start + m], named)
    names[0] = named

    def name_copies():
        yield remote(names.at[0], names.at[1], name_sem.at[0], name_sem.at[1], partner)
        for o in range(1, chips):
            for other in (0, 1):
                yield remote(names.at[0], names.at[2 * o + other], name_sem.at[0], name_sem.at[1], peer(o, not other))

    others = names.at[pl.ds(1, groups - 1)]
    all_names = remote(others, others, name_sem.at[0], name_sem.at[1], partner)

    for c in first_loads:
        c.wait()
    for c in later_loads:
        c.start()

    def first(i):
        value = damping * dot(smoother[i], rhs[i].astype(low))
        iterate[i] = value
        ext1[margin + i] = value.astype(low)

    for j in range(steps):
        rows(height - (j + 1) * chunk, chunk, first, 4)
        rows(j * chunk, chunk, first, 4)
        if j == 1:
            pl.semaphore_wait(barrier, met)
            push(depth)
            for c in name_copies():
                c.start()

    order = absorb_order(groups, steps)
    place_of = {key: 1 + sublanes * n for n, key in enumerate(order)}
    all_names.wait_recv()
    columns = jnp.zeros((sublanes, lanes), jnp.int32)
    places = []
    for k in range(groups):
        columns = jnp.where(sublane == k, names[k], columns)
        spot = lane % sublanes
        for j in range(steps):
            spot = jnp.where(lane // sublanes == j, spot + place_of[k, j], spot)
        places.append(spot)
    columns = columns.T
    found = [jnp.zeros((sublanes, lanes), jnp.int32) for _ in range(groups + 1)]
    for k in range(groups):
        for j in range(steps):
            column = jnp.broadcast_to(columns[sublanes * j : sublanes * (j + 1), k : k + 1], (sublanes, lanes))
            spot = place_of[k, j] + sublane
            for i in range(groups):
                hit = jnp.logical_and(column == names[i], spot < places[i])
                found[i] = jnp.maximum(found[i], jnp.where(hit, spot, 0))
            hit = column == r * cheight + lane
            found[groups] = jnp.maximum(found[groups], jnp.where(hit, spot, 0))
    for i in range(groups + 1):
        best = found[i]
        for shift in (1, 2, 4):
            best = jnp.maximum(best, pltpu.roll(best, shift, 0))
        tables[pl.ds(sublanes * i, sublanes)] = best
    to_scalar = load(tables, chain, 7)
    to_scalar.start()
    sums[0] = jnp.zeros(sums.shape[1:], f32)
    to_scalar.wait()
    later_loads[0].wait()
    later_loads[1].wait()

    base = flat * height - margin

    def residual_low(i):
        residual = rhs[i] - row_product(i, fine_cols, i, base, blocks, diag, ext1, margin + i)
        ext2[margin + i] = residual.astype(low)

    def second(i):
        value = iterate[i] + damping * dot(smoother[i], ext2[margin + i])
        iterate[i] = value
        ext2[margin + i] = value.astype(low)

    for j in range(steps):
        push(min(2 * j + 2 + depth, second_queue))
        wait_halo(0, j)
        for body in (residual_low, second):
            rows(margin - (j + 1) * chunk, chunk, body, 4)
            rows(margin + j * chunk, chunk, body, 4)
    push(second_queue + depth)

    def third(shift, spot):
        def body(i):
            at = i + shift
            residual = rhs[i] - row_product(i, fine_cols, i, base, blocks, diag, ext2, margin + i)
            own_full[at] = residual
            own_low[at] = residual.astype(low)
            sums[at + spot] = residual + sums[chain[0, at]]

        return body

    def near(j, count=sublanes):
        at = pl.ds(j * sublanes, count)
        return remote(own_full.at[at], near_full.at[at], near_send.at[0], near_recv.at[j], partner)

    def far(o, j, count=sublanes):
        at = pl.ds(j * sublanes, count)
        return remote(own_low.at[at], far_low.at[o - 1, at], far_send.at[o - 1], far_recv.at[o - 1, j], peer(o, True))

    def via(o, j, count=sublanes):
        at = pl.ds(j * sublanes, count)
        return remote(
            far_low.at[o - 1, at], via_low.at[o - 1, at], via_send.at[o - 1], via_recv.at[o - 1, j], partner
        )

    def absorb(k, j):
        source = near_full if k == 1 else (via_low if k % 2 else far_low).at[k // 2 - 1]
        spot = place_of[k, j] - j * sublanes

        def body(at):
            sums[at + spot] = source[at].astype(f32) + sums[chain[sublanes * k, at]]

        rows(j * sublanes, sublanes, body, 4)

    for k, j in order:
        o = k // 2
        if k == 0:
            push(second_queue + 2 * j + 2 + depth)
            wait_halo(1, j)
            for n in (0, 1):
                start, at = starts[2 * j + n], (2 * j + n) * chunk
                rows(start, chunk, third(at - start, place_of[k, j] - j * sublanes), 2)
            for o in range(1, chips):
                far(o, j).start()
            near(j).start()
        elif k == 1:
            near(j).wait_recv()
            absorb(k, j)
        elif k % 2 == 0:
            far(o, j).wait_recv()
            via(o, j).start()
            absorb(k, j)
        else:
            via(o, j).wait_recv()
            absorb(k, j)
    for c in later_loads[2:]:
        c.wait()

    def coarse_first(c):
        value = damping * dot(csmoother[c], sums[chain[sublanes * groups, c]].astype(low))
        cfirst[c] = value
        cext[cmargin + c] = value.astype(low)

    def spot_of(u):
        return side * (cmargin - (u + 1) * csub) + core * u * csub

    def across(p):
        at = spot_of(p * chips + chip)
        src = cext.at[pl.ds(cmargin + side * cmargin + at, csub)]
        return remote(src, clanding.at[pl.ds(at, csub)], cx_send.at[0], cx_recv.at[p], forth)

    def forward(o, p):
        at = pl.ds(spot_of(p * chips + chip), csub)
        return remote(clanding.at[at], clanding.at[at], cf_send.at[o - 1], cf_recv.at[o - 1, p], peer(o, True))

    for p in range(parts):
        rows(side * cmargin + spot_of(p * chips + chip), csub, coarse_first, csub)
        pl.when(can_send)(lambda: across(p).start())
    for p in range(parts):
        for o in range(1, chips):
            rows(side * cmargin + spot_of(p * chips + (chip + o) % chips), csub, coarse_first, csub)
    rows(core * cmargin, cmargin, coarse_first, 4)

    cbase = r * cheight - cmargin
    own = core * cmargin

    def coarse_residual(n):
        image = row_product(n, coarse_cols, own + n, cbase, cblocks, cdiag, cext, cmargin + own + n)
        cres[n] = (sums[chain[sublanes * groups, own + n]] - image).astype(low)

    def coarse_second(n):
        correction[own + n] = cfirst[own + n] + damping * dot(csmoother[own + n], cres[n])

    def back(p):
        at = pl.ds(own + side * (cmargin - (p + 1) * span) + core * p * span, span)
        return remote(correction.at[at], correction.at[at], cp_sem.at[0], cp_sem.at[1], partner)

    halves = correction.at[mine]
    all_back = remote(halves, halves, cp_sem.at[0], cp_sem.at[1], partner)
    sent = clanding.at[pl.ds(0, parts * csub)]
    all_across = remote(sent, sent, cx_send.at[0], cx_recv.at[0], forth)
    all_forward = [remote(sent, sent, cf_send.at[o - 1], cf_recv.at[o - 1, 0], peer(o, True)) for o in range(1, chips)]

    def receive(p):
        def go():
            across(p).wait_recv()
            for o in range(1, chips):
                forward(o, p).start()

        pl.when(can_recv)(go)

    receive(0)
    for p in range(parts):
        if p + 1 < parts:
            receive(p + 1)
        begin = side * (cmargin - (p + 1) * span) + core * p * span

        def arrived():
            for o in range(1, chips):
                forward(o, p).wait_recv()

            def place(n):
                cext[core * (cmargin + cheight) + n] = clanding[n]

            rows(begin, span, place, 4)

        pl.when(can_recv)(arrived)
        rows(begin, span, coarse_residual, 4)
        rows(begin, span, coarse_second, 4)
        back(p).start()
    all_back.wait_recv()

    cstart = r * cheight

    def final(i):
        iterate[i] = iterate[i] + correction[jnp.clip(aggregate[i] - cstart, 0, cheight - 1)]

    rows(0, height, final, 4)

    for n in range(len(queue) - depth, len(queue)):
        wait_sent(n)
    all_names.wait_send()
    near(0, height).wait_send()
    for o in range(1, chips):
        far(o, 0, height).wait_send()
        via(o, 0, height).wait_send()

    for c in all_forward:
        pl.when(can_recv)(lambda: c.wait_send())
    pl.when(can_send)(lambda: all_across.wait_send())
    all_back.wait_send()


def on_device(
    groups, ranks,
    rhs, fine_diag, fine_smoother, fine_blocks, fine_cols, aggregate,
    coarse_diag, coarse_smoother, coarse_blocks, coarse_cols,
):
    height, b, n = rhs.shape
    cheight = coarse_diag.shape[0]
    cmargin = cheight // 2
    neighbours = fine_blocks.shape[1]
    chips = groups // 2
    steps = height // sublanes
    parts = cmargin // (csub * chips)
    vmem = pltpu.VMEM
    dma = pltpu.SemaphoreType.DMA
    smem = pl.BlockSpec(memory_space=pltpu.SMEM)
    hbm = pl.BlockSpec(memory_space=pl.ANY)
    return pl.pallas_call(
        functools.partial(kernel, groups, ranks),
        out_shape=pltpu.VMEM(rhs.shape, f32),
        in_specs=[smem] * 3 + [hbm] * 7,
        out_specs=pl.BlockSpec(memory_space=pltpu.VMEM),
        scratch_shapes=[
            vmem((height, b, n), f32),
            vmem((height, b, b), low),
            vmem((height, b, b), low),
            vmem((height, neighbours, b, b), low),
            vmem((cmargin, b, b), low),
            vmem((cheight, b, b), low),
            vmem((cmargin, neighbours, b, b), low),
            vmem((2 * height, b, n), low),
            vmem((2 * height, b, n), low),
            vmem((2, height // 2, b, n), low),
            vmem((2, height // 2, b, n), low),
            vmem((height, b, n), f32),
            vmem((height, b, n), low),
            vmem((height, b, n), f32),
            vmem((chips - 1, height, b, n), low),
            vmem((chips - 1, height, b, n), low),
            vmem((groups * height + 1, b, n), f32),
            vmem((groups, sublanes, lanes), jnp.int32),
            vmem(((groups + 1) * sublanes, lanes), jnp.int32),
            pltpu.SMEM(((groups + 1) * sublanes, lanes), jnp.int32),
            vmem((cheight, b, n), f32),
            vmem((cmargin, b, n), low),
            vmem((2 * cheight, b, n), low),
            vmem((cmargin, b, n), low),
            vmem((cheight, b, n), f32),
            dma((8,)),
            dma((2, depth)),
            dma((2, 2, steps)),
            dma((2,)),
            dma((1,)),
            dma((steps,)),
            dma((chips - 1,)),
            dma((chips - 1, steps)),
            dma((chips - 1,)),
            dma((chips - 1, steps)),
            dma((1,)),
            dma((parts,)),
            dma((chips - 1,)),
            dma((chips - 1, parts)),
            dma((2,)),
        ],
        compiler_params=pltpu.CompilerParams(
            collective_id=0, has_side_effects=True, vmem_limit_bytes=58 * 1024 * 1024
        ),
        name="cycle",
    )(
        fine_cols.T, coarse_cols.T, aggregate,
        rhs, fine_diag, fine_smoother, fine_blocks, coarse_diag, coarse_smoother, coarse_blocks,
    )


def solution(mesh):
    fine = P(("grp", "rows"))
    return jax.shard_map(
        functools.partial(on_device, mesh.shape["grp"], mesh.shape["rows"]),
        mesh=mesh,
        in_specs=(fine,) * 6 + (P("rows"),) * 4,
        out_specs=fine,
        check_vma=False,
    )
```

time: 85.9 us -> 80.9 us (0.942)
  Pallas kernels: 85.2 us -> 79.4 us
  local copies, waits for them, and re-layouts: 0 us -> 1.32 us
    pallas_call x2 -> x1, Pallas kernels: 85.2 us -> 79.4 us  [on_device(): pl.pallas_call(functools.partial(kernel, groups, ranks), out_shape=pltpu....]
    unnamed x0 -> x1, local copies, waits for them, and re-layouts: none -> 1.32 us
where the time goes in v2:
time: 80.9 us; the launch traced here: 80.8 us
  Pallas kernels  79.4 us (98%)
  local copies, waits for them, and re-layouts  1.32 us (2%)
    pallas_call x1, Pallas kernels, on_device(): pl.pallas_call(functools.partial(kernel, groups, ranks), out_shape=pltpu....  79.4 us

profile of v2, /device:TPU:3, one launch (start us, length us, event | category | flops | bytes accessed | tf_op | source)
XLA Modules:
  0.0 80.8 jit_solution(13679364357856983408)
XLA Ops:
  0.0 79.4 %cycle.1 = f32[64,64,128]{2,1,0:T(8,128)S(1)} custom-call(s32[7,64]{1,0:T(8,128)} %bitcast.2, s32[7,64]{1,0:T(8,128)} %bitcast.3, s32[64]{0:T(128)} %aggregate.1, f32[64,64,128]{2,1,0:T(8,128)} %rhs_hbm.1, bf16[64,64,64]{2,1,0:T(8,128)(2,1)} %diag_hbm.1, bf16[64,64,64]{2,1,0:T(8,128)(2,1)} %smoother_hbm.1, bf16[64,7,64,64]{3,2,1,0:T(8,128)(2,1)} %blocks_hbm.1, ...), custom_call_target="tpu_custom_call" | custom-call | tf_op jit(solution)/shard_map/cycle/pallas_call | solution.py:433
  79.4 1.3 %copy.12 = f32[64,64,128]{2,1,0:T(8,128)} copy(f32[64,64,128]{2,1,0:T(8,128)S(1)} %cycle.1) | data formatting | bytes 4194304

commit v3 on v2

--- a/solution.py
+++ b/solution.py
@@ -12,7 +12,7 @@
 lanes = 128
 sublanes = 8
 depth = 4
-csub = 4
+csub = 2
 low = jnp.bfloat16
 f32 = jnp.float32
 
@@ -262,13 +262,11 @@
             rows(margin + j * chunk, chunk, body, 4)
     push(second_queue + depth)
 
-    def third(shift, spot):
+    def third(shift):
         def body(i):
-            at = i + shift
             residual = rhs[i] - row_product(i, fine_cols, i, base, blocks, diag, ext2, margin + i)
-            own_full[at] = residual
-            own_low[at] = residual.astype(low)
-            sums[at + spot] = residual + sums[chain[0, at]]
+            own_full[i + shift] = residual
+            own_low[i + shift] = residual.astype(low)
 
         return body
 
@@ -276,8 +274,8 @@
         at = pl.ds(j * sublanes, count)
         return remote(own_full.at[at], near_full.at[at], near_send.at[0], near_recv.at[j], partner)
 
-    def far(o, j, count=sublanes):
-        at = pl.ds(j * sublanes, count)
+    def far(o, begin, count, j=0):
+        at = pl.ds(begin, count)
         return remote(own_low.at[at], far_low.at[o - 1, at], far_send.at[o - 1], far_recv.at[o - 1, j], peer(o, True))
 
     def via(o, j, count=sublanes):
@@ -287,7 +285,7 @@
         )
 
     def absorb(k, j):
-        source = near_full if k == 1 else (via_low if k % 2 else far_low).at[k // 2 - 1]
+        source = (own_full, near_full)[k] if k < 2 else (via_low if k % 2 else far_low).at[k // 2 - 1]
         spot = place_of[k, j] - j * sublanes
 
         def body(at):
@@ -302,15 +300,16 @@
             wait_halo(1, j)
             for n in (0, 1):
                 start, at = starts[2 * j + n], (2 * j + n) * chunk
-                rows(start, chunk, third(at - start, place_of[k, j] - j * sublanes), 2)
-            for o in range(1, chips):
-                far(o, j).start()
+                rows(start, chunk, third(at - start), 4)
+                for o in range(1, chips):
+                    far(o, at, chunk, j).start()
             near(j).start()
+            absorb(k, j)
         elif k == 1:
             near(j).wait_recv()
             absorb(k, j)
         elif k % 2 == 0:
-            far(o, j).wait_recv()
+            far(o, j * sublanes, sublanes, j).wait_recv()
             via(o, j).start()
             absorb(k, j)
         else:
@@ -372,10 +371,9 @@
 
         pl.when(can_recv)(go)
 
-    receive(0)
     for p in range(parts):
-        if p + 1 < parts:
-            receive(p + 1)
+        receive(p)
+    for p in range(parts):
         begin = side * (cmargin - (p + 1) * span) + core * p * span
 
         def arrived():
@@ -385,7 +383,7 @@
             def place(n):
                 cext[core * (cmargin + cheight) + n] = clanding[n]
 
-            rows(begin, span, place, 4)
+            rows(begin, span, place, span)
 
         pl.when(can_recv)(arrived)
         rows(begin, span, coarse_residual, 4)

time: 80.9 us -> 77.9 us (0.963); the launches traced: 80.8 us -> 76.6 us
  Pallas kernels: 79.4 us -> 75.3 us
    pallas_call x1, Pallas kernels: 79.4 us -> 75.3 us  [on_device(): pl.pallas_call(functools.partial(kernel, groups, ranks), out_shape=pltpu....]
where the time goes in v3:
time: 77.9 us; the launch traced here: 76.6 us
  Pallas kernels  75.3 us (97%)
  local copies, waits for them, and re-layouts  1.32 us (2%)
    pallas_call x1, Pallas kernels, on_device(): pl.pallas_call(functools.partial(kernel, groups, ranks), out_shape=pltpu....  75.3 us

profile of v3, /device:TPU:3, one launch (start us, length us, event | category | flops | bytes accessed | tf_op | source)
XLA Modules:
  0.0 76.6 jit_solution(15931202779193151969)
XLA Ops:
  0.0 75.3 %cycle.1 = f32[64,64,128]{2,1,0:T(8,128)S(1)} custom-call(s32[7,64]{1,0:T(8,128)} %bitcast.2, s32[7,64]{1,0:T(8,128)} %bitcast.3, s32[64]{0:T(128)} %aggregate.1, f32[64,64,128]{2,1,0:T(8,128)} %rhs_hbm.1, bf16[64,64,64]{2,1,0:T(8,128)(2,1)} %diag_hbm.1, bf16[64,64,64]{2,1,0:T(8,128)(2,1)} %smoother_hbm.1, bf16[64,7,64,64]{3,2,1,0:T(8,128)(2,1)} %blocks_hbm.1, ...), custom_call_target="tpu_custom_call" | custom-call | tf_op jit(solution)/shard_map/cycle/pallas_call | solution.py:431
  75.3 1.3 %copy.12 = f32[64,64,128]{2,1,0:T(8,128)} copy(f32[64,64,128]{2,1,0:T(8,128)S(1)} %cycle.1) | data formatting | bytes 4194304

commit v4 on v3

v4 whole, which is shorter than its diff:
```python
import functools

import jax
import jax.numpy as jnp
from jax import lax
from jax.experimental import pallas as pl
from jax.experimental.pallas import tpu as pltpu
from jax.sharding import PartitionSpec as P

MESH = pl.DeviceIdType.MESH
damping = 0.8
lanes = 128
sublanes = 8
depth = 4
fewer = 3
later = 3
early = 8
csub = 2
low = jnp.bfloat16
f32 = jnp.float32


def dot(a, b):
    return jnp.dot(a, b, preferred_element_type=f32)


def row_product(i, columns, at, base, offs, diag, extended, own):
    count = offs.shape[1]
    last = extended.shape[0] - 1
    vectors = [extended[jnp.clip(columns[k, at] - base, 0, last)] for k in range(count)] + [extended[own]]
    blocks = [offs[i, k] for k in range(count)] + [diag[i]]
    total = None
    for p in range(0, count + 1, 4):
        term = dot(
            jnp.concatenate(blocks[p : p + 4], axis=1),
            jnp.concatenate(vectors[p : p + 4], axis=0),
        )
        total = term if total is None else total + term
    return total


def absorb_order(steps):
    order = [(k, t - k) for t in range(steps + 1) for k in (0, 1)]
    return [(k, j) for k, j in order if 0 <= j < steps]


def kernel(
    groups, ranks,
    fine_cols, coarse_cols, aggregate,
    rhs_hbm, diag_hbm, smoother_hbm, blocks_hbm, cdiag_hbm, csmoother_hbm, cblocks_hbm,
    iterate,
    rhs, diag, smoother, blocks, cdiag, csmoother, cblocks,
    ext1, ext2, landing1, landing2,
    own_full, near_full, sums, names, tables, chain,
    half_out, half_in, crhs, cfirst, cres, cext, clanding, correction,
    load_sem, halo_send, halo_recv, name_sem, near_send, near_recv,
    half_send, half_recv, cx_send, cx_recv, mate_sem, cp_sem,
):
    g = lax.axis_index("grp")
    r = lax.axis_index("rows")
    height = rhs.shape[0]
    margin = height // 2
    steps = height // sublanes
    chunk = sublanes // 2
    piece = chunk // 2
    cheight = correction.shape[0]
    cmargin = cheight // 2
    chips = groups // 2
    parts = cmargin // csub
    group = sublanes // csub

    flat = g * ranks + r
    has_left = flat > 0
    has_right = flat < groups * ranks - 1
    left = ((flat - 1) // ranks, (flat + ranks - 1) % ranks)
    right = ((flat + 1) // ranks, (flat + 1) % ranks)
    core = g % 2
    chip = g // 2
    partner = (chip * 2 + 1 - core, r)
    side = 1 - core
    forth = (chip * 2 + 1 - core, r - 1 + 2 * core)
    linked = jnp.where(core == 0, r > 0, r < ranks - 1)

    def peer(o):
        return (((chip + o) % chips) * 2 + core, r)

    def load(src, dst, at):
        return pltpu.make_async_copy(src, dst, load_sem.at[at])

    mine = pl.ds(core * cmargin, cmargin)
    first_loads = [load(rhs_hbm, rhs, 0), load(smoother_hbm, smoother, 1)]
    later_loads = [
        load(blocks_hbm, blocks, 2),
        load(diag_hbm, diag, 3),
        load(csmoother_hbm.at[mine], csmoother, 4),
        load(cdiag_hbm.at[mine], cdiag, 5),
        load(cblocks_hbm.at[mine], cblocks, 6),
    ]
    for c in first_loads:
        c.start()

    barrier = pltpu.get_barrier_semaphore()

    def greet(device):
        pl.semaphore_signal(barrier, inc=1, device_id=device, device_id_type=MESH)

    pl.when(has_left)(lambda: greet(left))
    pl.when(has_right)(lambda: greet(right))
    greet(partner)
    pl.when(linked)(lambda: greet(forth))
    for o in range(1, chips):
        greet(peer(o))
    met = chips + has_left.astype(jnp.int32) + has_right.astype(jnp.int32) + linked.astype(jnp.int32)

    def remote(src, dst, send, recv, device):
        return pltpu.make_async_remote_copy(
            src_ref=src, dst_ref=dst, send_sem=send, recv_sem=recv, device_id=device, device_id_type=MESH
        )

    pieces = margin // piece
    queue = [(0, j * piece, piece) for j in range(pieces)] + [(1, margin - piece, piece)]
    queue += [(1, j * piece, piece) for j in range(pieces - 1)]
    second_queue = pieces + 1
    pushed, drained = [], []
    exts, landings = (ext1, ext2), (landing1, landing2)

    def to_right(n, item=None):
        phase, start, count = item or queue[n]
        src = exts[phase].at[pl.ds(margin + height - start - count, count)]
        dst = landings[phase].at[0, pl.ds(margin - start - count, count)]
        return remote(src, dst, halo_send.at[0, n % depth], halo_recv.at[phase, 0, start // chunk], right)

    def to_left(n, item=None):
        phase, start, count = item or queue[n]
        src = exts[phase].at[pl.ds(margin + start, count)]
        dst = landings[phase].at[1, pl.ds(start, count)]
        return remote(src, dst, halo_send.at[1, n % depth], halo_recv.at[phase, 1, start // chunk], left)

    def wait_sent(n):
        pl.when(has_right)(lambda: to_right(n).wait_send())
        pl.when(has_left)(lambda: to_left(n).wait_send())

    def launch(n):
        if n < second_queue:
            window = depth
        else:
            window = fewer if n < second_queue + 4 else later
        while len(drained) <= n - window:
            wait_sent(len(drained))
            drained.append(None)
        pl.when(has_right)(lambda: to_right(n).start())
        pl.when(has_left)(lambda: to_left(n).start())

    def push(upto):
        while len(pushed) < min(upto, len(queue)):
            launch(len(pushed))
            pushed.append(None)

    def rows(start, count, body, unroll):
        def step(n, carry):
            body(start + n)
            return carry

        lax.fori_loop(0, count, step, 0, unroll=unroll)

    def wait_halo(phase, j):
        start, count = j * chunk, chunk
        pl.when(has_left)(lambda: to_right(0, (phase, start, count)).wait_recv())
        pl.when(has_right)(lambda: to_left(0, (phase, start, count)).wait_recv())
        ext, landing = exts[phase], landings[phase]

        def place_low(i):
            ext[i] = landing[0, i]

        def place_high(i):
            ext[margin + height + i] = landing[1, i]

        pl.when(has_left)(lambda: rows(margin - start - count, count, place_low, count))
        pl.when(has_right)(lambda: rows(start, count, place_high, count))

    starts = [at for j in range(steps) for at in (margin - (j + 1) * chunk, margin + j * chunk)]

    lane = lax.broadcasted_iota(jnp.int32, (sublanes, lanes), 1)
    sublane = lax.broadcasted_iota(jnp.int32, (sublanes, lanes), 0)
    named = jnp.zeros((sublanes, lanes), jnp.int32)
    for n, start in enumerate(starts):
        for m in range(chunk):
            named = jnp.where(lane == n * chunk + m, aggregate[start + m], named)
    names[0] = named

    name_copy = remote(names.at[0], names.at[1], name_sem.at[0], name_sem.at[1], partner)

    for c in first_loads:
        c.wait()
    for c in later_loads:
        c.start()

    def first(i):
        value = damping * dot(smoother[i], rhs[i].astype(low))
        iterate[i] = value
        ext1[margin + i] = value.astype(low)

    for j in range(steps):
        rows(height - (j + 1) * chunk, chunk, first, 4)
        rows(j * chunk, chunk, first, 4)
        if j == 1:
            pl.semaphore_wait(barrier, met)
            push(depth)
            name_copy.start()

    order = absorb_order(steps)
    place_of = {key: 1 + sublanes * n for n, key in enumerate(order)}
    name_copy.wait_recv()
    columns = jnp.zeros((sublanes, lanes), jnp.int32)
    places = []
    for k in (0, 1):
        columns = jnp.where(sublane == k, names[k], columns)
        spot = lane % sublanes
        for j in range(steps):
            spot = jnp.where(lane // sublanes == j, spot + place_of[k, j], spot)
        places.append(spot)
    columns = columns.T
    found = [jnp.zeros((sublanes, lanes), jnp.int32) for _ in range(3)]
    for k in (0, 1):
        for j in range(steps):
            column = jnp.broadcast_to(columns[sublanes * j : sublanes * (j + 1), k : k + 1], (sublanes, lanes))
            spot = place_of[k, j] + sublane
            for i in (0, 1):
                hit = jnp.logical_and(column == names[i], spot < places[i])
                found[i] = jnp.maximum(found[i], jnp.where(hit, spot, 0))
            hit = column == r * cheight + lane
            found[2] = jnp.maximum(found[2], jnp.where(hit, spot, 0))
    for i in range(3):
        best = found[i]
        for shift in (1, 2, 4):
            best = jnp.maximum(best, pltpu.roll(best, shift, 0))
        tables[pl.ds(sublanes * i, sublanes)] = best
    to_scalar = load(tables, chain, 7)
    to_scalar.start()
    sums[0] = jnp.zeros(sums.shape[1:], f32)
    to_scalar.wait()
    later_loads[0].wait()
    later_loads[1].wait()

    base = flat * height - margin

    def residual_low(i):
        residual = rhs[i] - row_product(i, fine_cols, i, base, blocks, diag, ext1, margin + i)
        ext2[margin + i] = residual.astype(low)

    def second(i):
        value = iterate[i] + damping * dot(smoother[i], ext2[margin + i])
        iterate[i] = value
        ext2[margin + i] = value.astype(low)

    for j in range(steps):
        push(min(2 * j + 2 + depth, second_queue))
        wait_halo(0, j)
        for body in (residual_low, second):
            for n in range(sublanes):
                body(starts[2 * j + n // chunk] + n % chunk)
    push(second_queue + 2)

    def third(i, at):
        residual = rhs[i] - row_product(i, fine_cols, i, base, blocks, diag, ext2, margin + i)
        own_full[at] = residual

    def near(j, count=sublanes):
        at = pl.ds(j * sublanes, count)
        return remote(own_full.at[at], near_full.at[at], near_send.at[0], near_recv.at[j], partner)

    def absorb(k, j):
        source = (own_full, near_full)[k]
        spot = place_of[k, j] - j * sublanes

        def body(at):
            sums[at + spot] = source[at] + sums[chain[sublanes * k, at]]

        rows(j * sublanes, sublanes, body, 4)

    for k, j in order:
        if k == 0:
            push(second_queue + 2 * j + 2 + later)
            wait_halo(1, j)
            for n in range(sublanes):
                third(starts[2 * j + n // chunk] + n % chunk, j * sublanes + n)
            near(j).start()
        else:
            near(j).wait_recv()
        absorb(k, j)

    own = core * cmargin

    def whole(n):
        return sums[chain[2 * sublanes, own + n]]

    def begin(p):
        return core * (cmargin - (p + 1) * csub) + side * p * csub

    def half(o, p, count=csub):
        at = pl.ds(p * csub, count)
        return remote(half_out.at[at], half_in.at[o - 1, at], half_send.at[o - 1], half_recv.at[o - 1, p], peer(o))

    def share(p):
        for n in range(csub):
            half_out[p * csub + n] = whole(begin(p) + n).astype(low)
        for o in range(1, chips):
            half(o, p).start()

    for p in range(early):
        share(p)
    for c in later_loads[2:]:
        c.wait()

    def across(p):
        src = cext.at[pl.ds(cmargin + own + begin(p), csub)]
        return remote(src, clanding.at[pl.ds(begin(p), csub)], cx_send.at[0], cx_recv.at[p], forth)

    def mate(p):
        at = pl.ds(cmargin + own + begin(p), csub)
        return remote(cext.at[at], cext.at[at], mate_sem.at[0], mate_sem.at[1], partner)

    for p in range(parts):
        if p + early < parts:
            share(p + early)
        for o in range(1, chips):
            half(o, p).wait_recv()
        for m in range(csub):
            n = begin(p) + m
            total = whole(n)
            for o in range(1, chips):
                total = total + half_in[o - 1, p * csub + m].astype(f32)
            crhs[n] = total
            value = damping * dot(csmoother[n], total.astype(low))
            cfirst[n] = value
            cext[cmargin + own + n] = value.astype(low)
        pl.when(linked)(lambda: across(p).start())
        mate(p).start()

    cbase = r * cheight - cmargin

    def coarse_residual(n):
        image = row_product(n, coarse_cols, own + n, cbase, cblocks, cdiag, cext, cmargin + own + n)
        cres[n] = (crhs[n] - image).astype(low)

    def coarse_second(n):
        correction[own + n] = cfirst[n] + damping * dot(csmoother[n], cres[n])

    def back(k):
        at = pl.ds(own + side * (cmargin - (k + 1) * sublanes) + core * k * sublanes, sublanes)
        return remote(correction.at[at], correction.at[at], cp_sem.at[0], cp_sem.at[1], partner)

    halves = correction.at[mine]
    all_back = remote(halves, halves, cp_sem.at[0], cp_sem.at[1], partner)
    all_mate = remote(clanding, clanding, mate_sem.at[0], mate_sem.at[1], partner)
    all_across = remote(clanding, clanding, cx_send.at[0], cx_recv.at[0], forth)
    all_mate.wait_recv()
    for k in range(parts // group):
        first_row = side * (cmargin - (k + 1) * sublanes) + core * k * sublanes

        def arrived():
            for p in range(k * group, (k + 1) * group):
                across(p).wait_recv()

            def place(n):
                cext[core * (cmargin + cheight) + n] = clanding[n]

            rows(first_row, sublanes, place, 4)

        pl.when(linked)(arrived)
        for body in (coarse_residual, coarse_second):
            for n in range(sublanes):
                body(first_row + n)
        back(k).start()
    all_back.wait_recv()

    cstart = r * cheight

    def final(i):
        iterate[i] = iterate[i] + correction[jnp.clip(aggregate[i] - cstart, 0, cheight - 1)]

    rows(0, height, final, 4)

    for n in range(len(drained), len(queue)):
        wait_sent(n)
    name_copy.wait_send()
    near(0, height).wait_send()
    for o in range(1, chips):
        half(o, 0, cmargin).wait_send()

    pl.when(linked)(lambda: all_across.wait_send())
    all_mate.wait_send()
    all_back.wait_send()


def on_device(
    groups, ranks,
    rhs, fine_diag, fine_smoother, fine_blocks, fine_cols, aggregate,
    coarse_diag, coarse_smoother, coarse_blocks, coarse_cols,
):
    height, b, n = rhs.shape
    cheight = coarse_diag.shape[0]
    cmargin = cheight // 2
    neighbours = fine_blocks.shape[1]
    chips = groups // 2
    steps = height // sublanes
    parts = cmargin // csub
    vmem = pltpu.VMEM
    dma = pltpu.SemaphoreType.DMA
    smem = pl.BlockSpec(memory_space=pltpu.SMEM)
    hbm = pl.BlockSpec(memory_space=pl.ANY)
    return pl.pallas_call(
        functools.partial(kernel, groups, ranks),
        out_shape=pltpu.VMEM(rhs.shape, f32),
        in_specs=[smem] * 3 + [hbm] * 7,
        out_specs=pl.BlockSpec(memory_space=pltpu.VMEM),
        scratch_shapes=[
            vmem((height, b, n), f32),
            vmem((height, b, b), low),
            vmem((height, b, b), low),
            vmem((height, neighbours, b, b), low),
            vmem((cmargin, b, b), low),
            vmem((cmargin, b, b), low),
            vmem((cmargin, neighbours, b, b), low),
            vmem((2 * height, b, n), low),
            vmem((2 * height, b, n), low),
            vmem((2, height // 2, b, n), low),
            vmem((2, height // 2, b, n), low),
            vmem((height, b, n), f32),
            vmem((height, b, n), f32),
            vmem((2 * height + 1, b, n), f32),
            vmem((2, sublanes, lanes), jnp.int32),
            vmem((3 * sublanes, lanes), jnp.int32),
            pltpu.SMEM((3 * sublanes, lanes), jnp.int32),
            vmem((cmargin, b, n), low),
            vmem((chips - 1, cmargin, b, n), low),
            vmem((cmargin, b, n), f32),
            vmem((cmargin, b, n), f32),
            vmem((cmargin, b, n), low),
            vmem((2 * cheight, b, n), low),
            vmem((cmargin, b, n), low),
            vmem((cheight, b, n), f32),
            dma((8,)),
            dma((2, depth)),
            dma((2, 2, steps)),
            dma((2,)),
            dma((1,)),
            dma((steps,)),
            dma((chips - 1,)),
            dma((chips - 1, parts)),
            dma((1,)),
            dma((parts,)),
            dma((2,)),
            dma((2,)),
        ],
        compiler_params=pltpu.CompilerParams(
            collective_id=0, has_side_effects=True, vmem_limit_bytes=58 * 1024 * 1024
        ),
        name="cycle",
    )(
        fine_cols.T, coarse_cols.T, aggregate,
        rhs, fine_diag, fine_smoother, fine_blocks, coarse_diag, coarse_smoother, coarse_blocks,
    )


def solution(mesh):
    fine = P(("grp", "rows"))
    return jax.shard_map(
        functools.partial(on_device, mesh.shape["grp"], mesh.shape["rows"]),
        mesh=mesh,
        in_specs=(fine,) * 6 + (P("rows"),) * 4,
        out_specs=fine,
        check_vma=False,
    )
```

time: 77.9 us -> 75.3 us (0.967)
  Pallas kernels: 75.3 us -> 72.6 us
    pallas_call x1, Pallas kernels: 75.3 us -> 72.6 us  [on_device(): pl.pallas_call(functools.partial(kernel, groups, ranks), out_shape=pltpu....]
where the time goes in v4:
time: 75.3 us; the launch traced here: 73.9 us
  Pallas kernels  72.6 us (96%)
  local copies, waits for them, and re-layouts  1.32 us (2%)
    pallas_call x1, Pallas kernels, on_device(): pl.pallas_call(functools.partial(kernel, groups, ranks), out_shape=pltpu....  72.6 us

profile of v4, /device:TPU:3, one launch (start us, length us, event | category | flops | bytes accessed | tf_op | source)
XLA Modules:
  0.0 73.9 jit_solution(11911496748260023353)
XLA Ops:
  0.0 72.6 %cycle.1 = f32[64,64,128]{2,1,0:T(8,128)S(1)} custom-call(s32[7,64]{1,0:T(8,128)} %bitcast.2, s32[7,64]{1,0:T(8,128)} %bitcast.3, s32[64]{0:T(128)} %aggregate.1, f32[64,64,128]{2,1,0:T(8,128)} %rhs_hbm.1, bf16[64,64,64]{2,1,0:T(8,128)(2,1)} %diag_hbm.1, bf16[64,64,64]{2,1,0:T(8,128)(2,1)} %smoother_hbm.1, bf16[64,7,64,64]{3,2,1,0:T(8,128)(2,1)} %blocks_hbm.1, ...), custom_call_target="tpu_custom_call" | custom-call | tf_op jit(solution)/shard_map/cycle/pallas_call | solution.py:412
  72.6 1.3 %copy.12 = f32[64,64,128]{2,1,0:T(8,128)} copy(f32[64,64,128]{2,1,0:T(8,128)S(1)} %cycle.1) | data formatting | bytes 4194304

commit v5 on v4

--- a/solution.py
+++ b/solution.py
@@ -11,9 +11,9 @@
 damping = 0.8
 lanes = 128
 sublanes = 8
-depth = 4
+depth = 8
 fewer = 3
-later = 3
+later = 4
 early = 8
 csub = 2
 low = jnp.bfloat16
@@ -24,17 +24,19 @@
     return jnp.dot(a, b, preferred_element_type=f32)
 
 
-def row_product(i, columns, at, base, offs, diag, extended, own):
-    count = offs.shape[1]
+def pack(i, offs, diag, packed):
+    packed[i] = jnp.concatenate([offs[i, k] for k in range(offs.shape[1])] + [diag[i]], axis=1)
+
+
+def row_product(i, columns, at, base, packed, extended, own):
+    count = columns.shape[0]
+    width = packed.shape[2] // (count + 1)
     last = extended.shape[0] - 1
     vectors = [extended[jnp.clip(columns[k, at] - base, 0, last)] for k in range(count)] + [extended[own]]
-    blocks = [offs[i, k] for k in range(count)] + [diag[i]]
     total = None
     for p in range(0, count + 1, 4):
-        term = dot(
-            jnp.concatenate(blocks[p : p + 4], axis=1),
-            jnp.concatenate(vectors[p : p + 4], axis=0),
-        )
+        group = vectors[p : p + 4]
+        term = dot(packed[i, :, width * p : width * (p + len(group))], jnp.concatenate(group, axis=0))
         total = term if total is None else total + term
     return total
 
@@ -49,7 +51,7 @@
     fine_cols, coarse_cols, aggregate,
     rhs_hbm, diag_hbm, smoother_hbm, blocks_hbm, cdiag_hbm, csmoother_hbm, cblocks_hbm,
     iterate,
-    rhs, diag, smoother, blocks, cdiag, csmoother, cblocks,
+    rhs, diag, smoother, blocks, cdiag, csmoother, cblocks, packed, cpacked,
     ext1, ext2, landing1, landing2,
     own_full, near_full, sums, names, tables, chain,
     half_out, half_in, crhs, cfirst, cres, cext, clanding, correction,
@@ -88,7 +90,11 @@
         return pltpu.make_async_copy(src, dst, load_sem.at[at])
 
     mine = pl.ds(core * cmargin, cmargin)
-    first_loads = [load(rhs_hbm, rhs, 0), load(smoother_hbm, smoother, 1)]
+    edge = sublanes
+    pairs = [(rhs_hbm, rhs), (smoother_hbm, smoother)]
+    spans = [pl.ds(0, edge), pl.ds(height - edge, edge), pl.ds(edge, height - 2 * edge)]
+    edge_loads = [load(a.at[at], b.at[at], 8 + 2 * n + m) for n, at in enumerate(spans[:2]) for m, (a, b) in enumerate(pairs)]
+    first_loads = [load(a.at[spans[2]], b.at[spans[2]], m) for m, (a, b) in enumerate(pairs)]
     later_loads = [
         load(blocks_hbm, blocks, 2),
         load(diag_hbm, diag, 3),
@@ -96,7 +102,7 @@
         load(cdiag_hbm.at[mine], cdiag, 5),
         load(cblocks_hbm.at[mine], cblocks, 6),
     ]
-    for c in first_loads:
+    for c in edge_loads + first_loads:
         c.start()
 
     barrier = pltpu.get_barrier_semaphore()
@@ -128,13 +134,13 @@
         phase, start, count = item or queue[n]
         src = exts[phase].at[pl.ds(margin + height - start - count, count)]
         dst = landings[phase].at[0, pl.ds(margin - start - count, count)]
-        return remote(src, dst, halo_send.at[0, n % depth], halo_recv.at[phase, 0, start // chunk], right)
+        return remote(src, dst, halo_send.at[0, n % depth], halo_recv.at[phase, start // chunk], right)
 
     def to_left(n, item=None):
         phase, start, count = item or queue[n]
         src = exts[phase].at[pl.ds(margin + start, count)]
         dst = landings[phase].at[1, pl.ds(start, count)]
-        return remote(src, dst, halo_send.at[1, n % depth], halo_recv.at[phase, 1, start // chunk], left)
+        return remote(src, dst, halo_send.at[1, n % depth], halo_recv.at[phase, start // chunk], left)
 
     def wait_sent(n):
         pl.when(has_right)(lambda: to_right(n).wait_send())
@@ -165,9 +171,12 @@
 
     def wait_halo(phase, j):
         start, count = j * chunk, chunk
-        pl.when(has_left)(lambda: to_right(0, (phase, start, count)).wait_recv())
-        pl.when(has_right)(lambda: to_left(0, (phase, start, count)).wait_recv())
         ext, landing = exts[phase], landings[phase]
+        sides = landing.at[:, pl.ds(start, count)]
+        both = remote(sides, sides, halo_send.at[0, 0], halo_recv.at[phase, j], left)
+        pl.when(jnp.logical_and(has_left, has_right))(lambda: both.wait_recv())
+        pl.when(jnp.logical_not(has_right))(lambda: to_right(0, (phase, start, count)).wait_recv())
+        pl.when(jnp.logical_not(has_left))(lambda: to_left(0, (phase, start, count)).wait_recv())
 
         def place_low(i):
             ext[i] = landing[0, i]
@@ -190,10 +199,8 @@
 
     name_copy = remote(names.at[0], names.at[1], name_sem.at[0], name_sem.at[1], partner)
 
-    for c in first_loads:
+    for c in edge_loads:
         c.wait()
-    for c in later_loads:
-        c.start()
 
     def first(i):
         value = damping * dot(smoother[i], rhs[i].astype(low))
@@ -205,9 +212,15 @@
         rows(j * chunk, chunk, first, 4)
         if j == 1:
             pl.semaphore_wait(barrier, met)
-            push(depth)
-            name_copy.start()
-
+            push(2 * j + 2)
+            for c in first_loads:
+                c.wait()
+            for c in later_loads:
+                c.start()
+
+        elif 1 < j and 2 * j + 2 <= depth:
+            push(2 * j + 2)
+    name_copy.start()
     order = absorb_order(steps)
     place_of = {key: 1 + sublanes * n for n, key in enumerate(order)}
     name_copy.wait_recv()
@@ -245,7 +258,7 @@
     base = flat * height - margin
 
     def residual_low(i):
-        residual = rhs[i] - row_product(i, fine_cols, i, base, blocks, diag, ext1, margin + i)
+        residual = rhs[i] - row_product(i, fine_cols, i, base, packed, ext1, margin + i)
         ext2[margin + i] = residual.astype(low)
 
     def second(i):
@@ -253,8 +266,22 @@
         iterate[i] = value
         ext2[margin + i] = value.astype(low)
 
+    def pack_step(j):
+        for start in starts[2 * j : 2 * j + 2]:
+            rows(start, chunk, lambda i: pack(i, blocks, diag, packed), 2)
+
+    pack_step(0)
+    pack_step(1)
     for j in range(steps):
         push(min(2 * j + 2 + depth, second_queue))
+        if j + 2 < steps:
+            pack_step(j + 2)
+        if j == 1:
+            for c in later_loads[2:]:
+                c.wait()
+        if 1 <= j < 5:
+            share_rows = cmargin // 4
+            rows((j - 1) * share_rows, share_rows, lambda i: pack(i, cblocks, cdiag, cpacked), 2)
         wait_halo(0, j)
         for body in (residual_low, second):
             for n in range(sublanes):
@@ -262,7 +289,7 @@
     push(second_queue + 2)
 
     def third(i, at):
-        residual = rhs[i] - row_product(i, fine_cols, i, base, blocks, diag, ext2, margin + i)
+        residual = rhs[i] - row_product(i, fine_cols, i, base, packed, ext2, margin + i)
         own_full[at] = residual
 
     def near(j, count=sublanes):
@@ -309,9 +336,6 @@
 
     for p in range(early):
         share(p)
-    for c in later_loads[2:]:
-        c.wait()
-
     def across(p):
         src = cext.at[pl.ds(cmargin + own + begin(p), csub)]
         return remote(src, clanding.at[pl.ds(begin(p), csub)], cx_send.at[0], cx_recv.at[p], forth)
@@ -340,14 +364,14 @@
     cbase = r * cheight - cmargin
 
     def coarse_residual(n):
-        image = row_product(n, coarse_cols, own + n, cbase, cblocks, cdiag, cext, cmargin + own + n)
+        image = row_product(n, coarse_cols, own + n, cbase, cpacked, cext, cmargin + own + n)
         cres[n] = (crhs[n] - image).astype(low)
 
     def coarse_second(n):
         correction[own + n] = cfirst[n] + damping * dot(csmoother[n], cres[n])
 
-    def back(k):
-        at = pl.ds(own + side * (cmargin - (k + 1) * sublanes) + core * k * sublanes, sublanes)
+    def back(row):
+        at = pl.ds(own + row, chunk)
         return remote(correction.at[at], correction.at[at], cp_sem.at[0], cp_sem.at[1], partner)
 
     halves = correction.at[mine]
@@ -368,10 +392,12 @@
             rows(first_row, sublanes, place, 4)
 
         pl.when(linked)(arrived)
-        for body in (coarse_residual, coarse_second):
-            for n in range(sublanes):
-                body(first_row + n)
-        back(k).start()
+        for n in range(sublanes):
+            coarse_residual(first_row + n)
+        for quarter in range(0, sublanes, chunk):
+            for n in range(chunk):
+                coarse_second(first_row + quarter + n)
+            back(first_row + quarter).start()
     all_back.wait_recv()
 
     cstart = r * cheight
@@ -422,6 +448,8 @@
             vmem((cmargin, b, b), low),
             vmem((cmargin, b, b), low),
             vmem((cmargin, neighbours, b, b), low),
+            vmem((height, b, (neighbours + 1) * b), low),
+            vmem((cmargin, b, (neighbours + 1) * b), low),
             vmem((2 * height, b, n), low),
             vmem((2 * height, b, n), low),
             vmem((2, height // 2, b, n), low),
@@ -440,9 +468,9 @@
             vmem((2 * cheight, b, n), low),
             vmem((cmargin, b, n), low),
             vmem((cheight, b, n), f32),
-            dma((8,)),
+            dma((12,)),
             dma((2, depth)),
-            dma((2, 2, steps)),
+            dma((2, steps)),
             dma((2,)),
             dma((1,)),
             dma((steps,)),

time: 75.3 us -> 74.8 us (level)
  no operation moved by 1% of the time
where the time goes in v5:
time: 74.8 us; the launch traced here: 74 us
  Pallas kernels  72.6 us (97%)
  local copies, waits for them, and re-layouts  1.32 us (2%)
    pallas_call x1, Pallas kernels, on_device(): pl.pallas_call(functools.partial(kernel, groups, ranks), out_shape=pltpu....  72.6 us

profile of v5, /device:TPU:3, one launch (start us, length us, event | category | flops | bytes accessed | tf_op | source)
XLA Modules:
  0.0 74.0 jit_solution(11663959172083954764)
XLA Ops:
  0.0 72.6 %cycle.1 = f32[64,64,128]{2,1,0:T(8,128)S(1)} custom-call(s32[7,64]{1,0:T(8,128)} %bitcast.2, s32[7,64]{1,0:T(8,128)} %bitcast.3, s32[64]{0:T(128)} %aggregate.1, f32[64,64,128]{2,1,0:T(8,128)} %rhs_hbm.1, bf16[64,64,64]{2,1,0:T(8,128)(2,1)} %diag_hbm.1, bf16[64,64,64]{2,1,0:T(8,128)(2,1)} %smoother_hbm.1, bf16[64,7,64,64]{3,2,1,0:T(8,128)(2,1)} %blocks_hbm.1, ...), custom_call_target="tpu_custom_call" | custom-call | tf_op jit(solution)/shard_map/cycle/pallas_call | solution.py:438
  72.7 1.3 %copy.12 = f32[64,64,128]{2,1,0:T(8,128)} copy(f32[64,64,128]{2,1,0:T(8,128)S(1)} %cycle.1) | data formatting | bytes 4194304

commit v6 on v5

--- a/solution.py
+++ b/solution.py
@@ -283,10 +283,15 @@
             share_rows = cmargin // 4
             rows((j - 1) * share_rows, share_rows, lambda i: pack(i, cblocks, cdiag, cpacked), 2)
         wait_halo(0, j)
-        for body in (residual_low, second):
-            for n in range(sublanes):
-                body(starts[2 * j + n // chunk] + n % chunk)
-    push(second_queue + 2)
+        picks = [starts[2 * j + n // chunk] + n % chunk for n in range(sublanes)]
+        if j == steps - 1:
+            picks.sort(key=lambda i: min(i, height - 1 - i))
+        for batch in [picks] if j < steps - 1 else [picks[: 2 * piece], picks[2 * piece :]]:
+            for body in (residual_low, second):
+                for i in batch:
+                    body(i)
+            if j == steps - 1:
+                push(len(pushed) + 1)
 
     def third(i, at):
         residual = rhs[i] - row_product(i, fine_cols, i, base, packed, ext2, margin + i)

time: 74.8 us -> 74.8 us (level)
  no operation moved by 1% of the time
where the time goes in v6:
time: 74.8 us; the launch traced here: 73.9 us
  Pallas kernels  72.5 us (97%)
  local copies, waits for them, and re-layouts  1.32 us (2%)
    pallas_call x1, Pallas kernels, on_device(): pl.pallas_call(functools.partial(kernel, groups, ranks), out_shape=pltpu....  72.5 us

profile of v6, /device:TPU:3, one launch (start us, length us, event | category | flops | bytes accessed | tf_op | source)
XLA Modules:
  0.0 73.9 jit_solution(6116999867642750553)
XLA Ops:
  0.0 72.5 %cycle.1 = f32[64,64,128]{2,1,0:T(8,128)S(1)} custom-call(s32[7,64]{1,0:T(8,128)} %bitcast.2, s32[7,64]{1,0:T(8,128)} %bitcast.3, s32[64]{0:T(128)} %aggregate.1, f32[64,64,128]{2,1,0:T(8,128)} %rhs_hbm.1, bf16[64,64,64]{2,1,0:T(8,128)(2,1)} %diag_hbm.1, bf16[64,64,64]{2,1,0:T(8,128)(2,1)} %smoother_hbm.1, bf16[64,7,64,64]{3,2,1,0:T(8,128)(2,1)} %blocks_hbm.1, ...), custom_call_target="tpu_custom_call" | custom-call | tf_op jit(solution)/shard_map/cycle/pallas_call | solution.py:443
  72.5 1.3 %copy.12 = f32[64,64,128]{2,1,0:T(8,128)} copy(f32[64,64,128]{2,1,0:T(8,128)S(1)} %cycle.1) | data formatting | bytes 4194304
